TPU v7x, 32 devices: a whole 2x2x4 slice. The times are simulated.
32 devices in a mesh: row: 8 (over y, x, core), col: 4 (over z).
Axes of the slice: x: 2, y: 2, z: 4, core: 2. Of those that a mesh axis runs over, the one named last changes fastest.
Arguments:
- surface_height: float32 [2048, 2048], P('row', 'col'), may hold values from -1.2 to 1.2
- surface_potential: float32 [2048, 2048], P('row', 'col'), may hold values from -4 to 4
- velocity: float32 [3, 16, 1024, 1024], P(None, None, 'row', 'col'), may hold values from -1.25 to 1.25
Outputs:
- height_rate: float32 [2048, 2048], P('row', 'col')
- potential_rate: float32 [2048, 2048], P('row', 'col')
- velocity_next: float32 [3, 16, 1024, 1024], P(None, None, 'row', 'col')
All inputs are finite; a program needn't handle non-finite values.
Results may differ from a plain program's by a relative error of at most 0.00019.
Values sent between devices are 32-bit elements; how exact they have to be, the bound alone decides.
No kernel may reach another device: no remote copies, remote signals or barrier semaphores. Data moves between devices by JAX's collectives and lax.ppermute only.
A program may use at most 192 MiB of HBM per device.

v0:
```python
import jax
import jax.numpy as jnp
from jax import lax
from jax.sharding import PartitionSpec as P

NX = 2048
NY = 2048
COARSE = 2
GRAVITY = 1.0
SURFACE_STEP = 0.05
FLOW_STEP = 0.5
VISCOSITY = 0.2
DECAY_RATE = 0.05


def with_halo(x, sides, width):
    for axis, dim in sides:
        peers, length = (lax.axis_size(axis), x.shape[dim])
        up = [(i, (i + 1) % peers) for i in range(peers)]
        down = [(j, i) for i, j in up]
        last = lax.slice_in_dim(x, length - width, length, axis=dim)
        leading = lax.slice_in_dim(x, 0, width, axis=dim)
        before = lax.ppermute(last, axis, up)
        after = lax.ppermute(leading, axis, down)
        x = jnp.concatenate([before, x, after], axis=dim)
    return x


def wave_numbers(index, length):
    signed = jnp.where(index < length // 2, index, index - length)
    kept_mask = (jnp.abs(signed) <= length // 3).astype(jnp.float32)
    return (2.0 * jnp.pi / length * signed.astype(jnp.float32), kept_mask)


def coarsen(source):
    rows_out = source.shape[0] // COARSE
    cols_out = source.shape[1] // COARSE
    return source.reshape(rows_out, COARSE, cols_out, COARSE).mean(axis=(1, 3))


def flow_update(padded_flow, padded_load, surface_u, surface_v):
    depth_count = padded_flow.shape[1]
    level_mid = jnp.arange(depth_count, dtype=jnp.float32)[:, None, None] + 0.5
    drift_decay = jnp.exp(-2.0 * DECAY_RATE * level_mid)
    load_decay = jnp.exp(-DECAY_RATE * level_mid)

    def derivs(source, top_value):
        middle = source[:, 1:-1, 1:-1]
        above_cell = jnp.concatenate([top_value[None], middle[:-1]], axis=0)
        below_cell = jnp.concatenate([middle[1:], middle[-1:]], axis=0)
        east_side = source[:, 1:-1, 2:]
        west_side = source[:, 1:-1, :-2]
        north_side = source[:, 2:, 1:-1]
        south_side = source[:, :-2, 1:-1]
        laplace = (
            east_side + west_side + north_side + south_side + above_cell + below_cell - 6.0 * middle
        )
        return (
            middle,
            0.5 * (east_side - west_side),
            0.5 * (north_side - south_side),
            0.5 * (above_cell - below_cell),
            laplace,
        )

    u_mid, u_dx, u_dy, u_dz, u_lap = derivs(padded_flow[0], surface_u)
    v_mid, v_dx, v_dy, v_dz, v_lap = derivs(padded_flow[1], surface_v)
    w_mid, w_dx, w_dy, w_dz, w_lap = derivs(padded_flow[2], jnp.zeros_like(surface_u))
    vort_x = w_dy - v_dz
    vort_y = u_dz - w_dx
    vort_z = v_dx - u_dy
    drift_u = surface_u[None] * drift_decay
    drift_v = surface_v[None] * drift_decay
    load_x = 0.5 * (padded_load[1:-1, 2:] - padded_load[1:-1, :-2])[None] * load_decay
    load_y = 0.5 * (padded_load[2:, 1:-1] - padded_load[:-2, 1:-1])[None] * load_decay

    def advance(middle, slope_x, slope_y, slope_z, laplace, forcing):
        carried = u_mid * slope_x + v_mid * slope_y + w_mid * slope_z
        return middle + FLOW_STEP * (-carried + VISCOSITY * laplace + forcing)

    next_u = advance(u_mid, u_dx, u_dy, u_dz, u_lap, drift_v * vort_z - load_x)
    next_v = advance(v_mid, v_dx, v_dy, v_dz, v_lap, -drift_u * vort_z - load_y)
    next_w = advance(w_mid, w_dx, w_dy, w_dz, w_lap, drift_u * vort_y - drift_v * vort_x)
    return jnp.stack([next_u, next_v, next_w])


def product(form, left, right):
    return jnp.einsum(form, left, right, precision=lax.Precision.HIGHEST)


def complex_product(form, left_real, left_imag, right_real, right_imag):
    if left_imag is None:
        return (product(form, left_real, right_real), product(form, left_real, right_imag))
    out_real = product(form, left_real, right_real) - product(form, left_imag, right_imag)
    out_imag = product(form, left_real, right_imag) + product(form, left_imag, right_real)
    return (out_real, out_imag)


def tables(length, direction):
    index = jnp.arange(length, dtype=jnp.int32)
    angle = 2.0 * jnp.pi / length * (index[:, None] * index[None, :] % length).astype(jnp.float32)
    return (jnp.cos(angle), direction * jnp.sin(angle))


def twiddles(factor_one, factor_two, direction):
    total = factor_one * factor_two
    index_one = jnp.arange(factor_one, dtype=jnp.int32)
    index_two = jnp.arange(factor_two, dtype=jnp.int32)
    angle = (
        2.0 * jnp.pi / total * (index_one[:, None] * index_two[None, :] % total).astype(jnp.float32)
    )
    return (jnp.cos(angle), direction * jnp.sin(angle))


def transform(real_part, imag_part, direction, layout, real_only):
    if layout == "back":
        length = real_part.shape[1]
    else:
        length = real_part.shape[2]
    factor_one = 1 << (length.bit_length() - 1) // 2
    factor_two = length // factor_one
    cos_one, sin_one = tables(factor_one, direction)
    cos_two, sin_two = tables(factor_two, direction)
    twist_cos, twist_sin = twiddles(factor_one, factor_two, direction)
    batch_size = real_part.shape[0]
    if layout == "back":
        cross_len = real_part.shape[2]
        shape_four = (batch_size, factor_one, factor_two, cross_len)
        first_form = "banm,ak->bknm"
        second_form = "bknm,nq->bmqk"
        twist_cos = twist_cos[None, :, :, None]
        twist_sin = twist_sin[None, :, :, None]
        out_shape = (batch_size, cross_len, length)
    else:
        cross_len = real_part.shape[1]
        shape_four = (batch_size, cross_len, factor_one, factor_two)
        first_form = "bman,ak->bmkn"
        twist_cos = twist_cos[None, None]
        twist_sin = twist_sin[None, None]
        if layout == "front":
            second_form = "bmkn,nq->bqkm"
            out_shape = (batch_size, length, cross_len)
        else:
            second_form = "bmkn,nq->bmqk"
            out_shape = (batch_size, cross_len, length)
    left_real = real_part.reshape(shape_four)
    left_imag = None if imag_part is None else imag_part.reshape(shape_four)
    mid_real, mid_imag = complex_product(first_form, left_real, left_imag, cos_one, sin_one)
    turned_real = mid_real * twist_cos - mid_imag * twist_sin
    turned_imag = mid_real * twist_sin + mid_imag * twist_cos
    if real_only:
        result = product(second_form, turned_real, cos_two) - product(
            second_form, turned_imag, sin_two
        )
        return result.reshape(out_shape)
    out_real, out_imag = complex_product(second_form, turned_real, turned_imag, cos_two, sin_two)
    return (out_real.reshape(out_shape), out_imag.reshape(out_shape))


def scaled(pair_value, factor):
    return (pair_value[0] * factor, pair_value[1] * factor)


def turned(pair_value, factor):
    return (-factor * pair_value[1], factor * pair_value[0])


def unfold_half(full_real, full_imag, kept_modes):
    weights = jnp.where(jnp.arange(kept_modes, dtype=jnp.int32) == 0, 1.0, 2.0).astype(jnp.float32)[
        None, :, None
    ]
    padding = jnp.zeros((full_real.shape[0], NX - kept_modes, full_real.shape[2]), jnp.float32)
    return (
        jnp.concatenate([full_real * weights, padding], axis=1),
        jnp.concatenate([full_imag * weights, padding], axis=1),
    )


def local(surface_height, surface_potential, velocity):
    col_count = lax.axis_size("col")
    device_count = lax.axis_size("row") * col_count
    place = lax.axis_index("row") * col_count + lax.axis_index("col")
    kept_modes = (NX // 3 + device_count) // device_count * device_count
    modes_each = kept_modes // device_count
    kx_index = place * modes_each + jnp.arange(modes_each, dtype=jnp.int32)
    kx_values, kx_kept = wave_numbers(kx_index, NX)
    ky_values, ky_kept = wave_numbers(jnp.arange(NY, dtype=jnp.int32), NY)
    kx_grid = kx_values[:, None]
    ky_grid = ky_values[None, :]
    mask = kx_kept[:, None] * ky_kept[None, :]
    magnitude = jnp.sqrt(kx_grid * kx_grid + ky_grid * ky_grid)

    def forward(stacked):
        pencil = lax.all_to_all(stacked, "col", split_axis=1, concat_axis=2, tiled=True)
        wide_real, wide_imag = transform(pencil, None, -1.0, "front", False)
        slab_real, slab_imag = (
            lax.all_to_all(
                wide_real[:, :kept_modes], ("row", "col"), split_axis=1, concat_axis=2, tiled=True
            ),
            lax.all_to_all(
                wide_imag[:, :kept_modes], ("row", "col"), split_axis=1, concat_axis=2, tiled=True
            ),
        )
        spec_real, spec_imag = transform(slab_real, slab_imag, -1.0, "last", False)
        return (spec_real * mask, spec_imag * mask)

    def inverse(pair_list):
        spec_real = jnp.stack([pair_item[0] for pair_item in pair_list])
        spec_imag = jnp.stack([pair_item[1] for pair_item in pair_list])
        line_real, line_imag = transform(spec_real, spec_imag, 1.0, "last", False)
        full_real, full_imag = (
            lax.all_to_all(line_real, ("row", "col"), split_axis=2, concat_axis=1, tiled=True),
            lax.all_to_all(line_imag, ("row", "col"), split_axis=2, concat_axis=1, tiled=True),
        )
        full_real, full_imag = unfold_half(full_real, full_imag, kept_modes)
        pencil = transform(full_real, full_imag, 1.0, "back", True) / float(NX * NY)
        return lax.all_to_all(pencil, "col", split_axis=2, concat_axis=1, tiled=True)

    first_real, first_imag = forward(jnp.stack([surface_potential, surface_height]))
    pot_hat = (first_real[0], first_imag[0])
    height_hat = (first_real[1], first_imag[1])
    first_fields = inverse(
        [
            scaled(pot_hat, magnitude),
            scaled(pot_hat, magnitude * magnitude),
            scaled(pot_hat, magnitude * magnitude * magnitude),
            turned(pot_hat, kx_grid),
            turned(pot_hat, ky_grid),
            turned(height_hat, kx_grid),
            turned(height_hat, ky_grid),
        ]
    )
    vert_one = first_fields[0]
    curve_one = first_fields[1]
    cube_one = first_fields[2]
    pot_dx = first_fields[3]
    pot_dy = first_fields[4]
    height_dx = first_fields[5]
    height_dy = first_fields[6]
    second_pot = -surface_height * vert_one
    second_real, second_imag = forward(second_pot[None])
    second_hat = (second_real[0], second_imag[0])
    second_fields = inverse(
        [scaled(second_hat, magnitude), scaled(second_hat, magnitude * magnitude)]
    )
    vert_two = second_fields[0]
    curve_two = second_fields[1]
    third_pot = -surface_height * vert_two - 0.5 * surface_height * surface_height * curve_one
    third_real, third_imag = forward(third_pot[None])
    vert_three = inverse([scaled((third_real[0], third_imag[0]), magnitude)])[0]
    vertical = (
        vert_one
        + vert_two
        + vert_three
        + surface_height * (curve_one + curve_two)
        + 0.5 * surface_height * surface_height * cube_one
    )
    slope = height_dx * height_dx + height_dy * height_dy
    height_rate = -(height_dx * pot_dx + height_dy * pot_dy) + (1.0 + slope) * vertical
    potential_rate = (
        -GRAVITY * surface_height
        - 0.5 * (pot_dx * pot_dx + pot_dy * pot_dy)
        + 0.5 * (1.0 + slope) * vertical * vertical
    )
    pressure = GRAVITY * coarsen(surface_height + SURFACE_STEP * height_rate)
    surface_u = coarsen(pot_dx)
    surface_v = coarsen(pot_dy)
    depth_count = velocity.shape[1]
    stacked_block = jnp.concatenate(
        [velocity.reshape((3 * depth_count,) + velocity.shape[2:]), pressure[None]], axis=0
    )
    padded_block = with_halo(stacked_block, (("row", 1), ("col", 2)), 1)
    padded_flow = padded_block[:-1].reshape((3, depth_count) + padded_block.shape[1:])
    padded_load = padded_block[-1]
    velocity_next = flow_update(padded_flow, padded_load, surface_u, surface_v)
    return (height_rate, potential_rate, velocity_next)


def solution(mesh):
    placed = (P("row", "col"), P("row", "col"), P(None, None, "row", "col"))
    return jax.shard_map(
        local,
        mesh=mesh,
        in_specs=placed,
        out_specs=(P("row", "col"), P("row", "col"), P(None, None, "row", "col")),
        check_vma=False,
    )
```

profile of v0, /device:TPU:0, one launch (start us, length us, event | category | flops | bytes accessed | tf_op | source)
XLA Modules:
  0.0 1156.2 jit_solution(16676131962339563223)
XLA Ops:
  5.4 6.3 all-to-all-start
  12.0 25.5 %all-to-all-done = f32[2,256,512]{2,0,1:T(2,128)S(1)} async-done(((f32[2,256,512]{2,0,1:T(2,128)}), f32[2,256,512]{2,0,1:T(2,128)S(1)}, u32[]{:S(2)}, u32[]{:S(2)}) %all-to-all-start) | async-done | bytes 1048608 | tf_op jit(solution)/shard_map/all_to_all | solution.py:194
  47.2 6.8 fusion.71
  54.0 18.9 %subtract_bitcast_fusion.3 = f32[2,64,32,64]{3,1,2,0:T(8,128)S(1)} fusion(f32[64,2,64,32]{2,0,3,1:T(8,128)S(1)} %fusion.71, f32[2,64,32,64]{3,2,1,0:T(8,128)S(1)} %get-tuple-element.49), kind=kOutput, calls=%fused_computation.117 | convolution fusion | flops 201646080 | bytes 3145728 | tf_op jit(solution)/shard_map/bmkn,nq->bqkm/dot_general | solution.py:88
  81.9 8.4 fusion.69
  90.2 6.8 add_bitcast_fusion.3
  111.8 6.3 all-to-all-done.2
  134.8 9.1 multiply_reduce_fusion.4
  183.9 8.6 copy.815
  192.6 8.0 reshape.1235
  212.7 8.6 copy.820
  221.4 8.0 reshape.1237
  250.0 6.5 copy.663
  259.0 9.1 all-to-all-done.4
  274.2 7.1 reshape.1238
  281.2 6.5 copy.671
  294.1 14.8 %fusion.4 = f32[32,7,64,64]{3,0,2,1:T(8,128)} fusion(f32[7,32,64,64]{3,2,1,0:T(8,128)S(1)} %bitcast.784), kind=kOutput, calls=%fused_computation.7 | convolution fusion | flops 352335872 | bytes 7340032 | tf_op jit(solution)/shard_map/banm,ak->bknm/dot_general | solution.py:88
  308.9 14.9 %fusion.6 = f32[32,7,64,64]{3,0,2,1:T(8,128)} fusion(f32[7,32,64,64]{3,2,1,0:T(8,128)S(1)} %bitcast.785), kind=kOutput, calls=%fused_computation.9 | convolution fusion | flops 352335872 | bytes 7340032 | tf_op jit(solution)/shard_map/banm,ak->bknm/dot_general | solution.py:88
  324.3 15.1 %fusion.8 = f32[32,7,64,64]{3,0,2,1:T(8,128)} fusion(f32[7,32,64,64]{3,2,1,0:T(8,128)S(1)} %bitcast.786), kind=kOutput, calls=%fused_computation.11 | convolution fusion | flops 352335872 | bytes 7340032 | tf_op jit(solution)/shard_map/banm,ak->bknm/dot_general | solution.py:88
  339.5 22.3 %subtract_bitcast_fusion = (f32[7,32,64,64]{3,1,2,0:T(8,128)}, f32[7,32,64,64]{3,1,2,0:T(8,128)}) fusion(f32[32,64]{0,1:T(8,128)S(1)} %copy.677, f32[32,64]{0,1:T(8,128)S(1)} %copy.674, f32[32,7,64,64]{3,0,2,1:T(8,128)} %fusion.8, f32[32,7,64,64]{3,0,2,1:T(8,128)} %fusion.4, f32[32,7,64,64]{3,0,2,1:T(8,128)} %fusion.6, f32[7,32,64,64]{3,2,1,0:T(8,128)S(1)} %bitcast.787), kind=kOutput, calls=%fused_computation.6 | convolution fusion | flops 359675904 | bytes 22036480 | tf_op jit(solution)/shard_map/banm,ak->bknm/dot_general | solution.py:88
  361.8 12.5 %fusion = f32[64,7,32,64]{3,0,2,1:T(8,128)S(1)} fusion(f32[7,32,64,64]{3,1,2,0:T(8,128)} %get-tuple-element.33), kind=kOutput, calls=%fused_computation | convolution fusion | flops 704700416 | bytes 7340032 | tf_op jit(solution)/shard_map/bknm,nq->bmqk/dot_general | solution.py:88
  374.3 11.4 multiply_bitcast_fusion
  390.3 12.8 %copy.1009 = f32[7,64,2048]{1,0,2:T(8,128)} copy(f32[7,64,2048]{1,2,0:T(8,128)S(1)} %bitcast.794) | data formatting | bytes 7340032 | tf_op jit(solution)/shard_map/div | solution.py:216
  403.1 8.2 reshape.1239
  411.3 88.3 %all_to_all.288 = f32[4,1,229376]{2,1,0:T(1,128)} all-to-all(f32[4,1,229376]{2,1,0:T(1,128)} %reshape.1239), channel_id=1, replica_groups=mesh['row'=8,'col'=4] {'col'}, dimensions={0} | all-to-all | bytes 7340032 | tf_op jit(solution)/shard_map/all_to_all | solution.py:217
  499.6 13.7 %reduce.32 = f32[4,229376]{1,0:T(4,128)} reduce(f32[4,1,229376]{2,1,0:T(1,128)} %all_to_all.288, f32[]{:T(128)} %broadcast.1607), dimensions={1}, to_apply=%all_to_all.227.reduce_sub_computation | reduce | bytes 7340036 | tf_op jit(solution)/shard_map/all_to_all | solution.py:217
  513.3 9.0 reshape.1240
  522.3 6.5 copy.683
  538.0 15.4 %all-to-all-done.6 = f32[1,256,512]{2,0,1:T(1,128)S(1)} async-done(((f32[1,256,512]{2,0,1:T(1,128)}), f32[1,256,512]{2,0,1:T(1,128)S(1)}, u32[]{:S(2)}, u32[]{:S(2)}) %all-to-all-start.6) | async-done | bytes 524320 | tf_op jit(solution)/shard_map/all_to_all | solution.py:194
  592.8 6.5 all-to-all-done.8
  692.6 8.6 copy.1010
  705.0 30.3 %all_to_all.289 = f32[4,1,65536]{2,1,0:T(1,128)} all-to-all(f32[4,1,65536]{2,1,0:T(1,128)S(1)} %reshape.1249), channel_id=1, replica_groups=mesh['row'=8,'col'=4] {'col'}, dimensions={0} | all-to-all | bytes 2097152 | tf_op jit(solution)/shard_map/all_to_all | solution.py:217
  747.7 17.4 %all_to_all.290 = f32[1,256,512]{2,0,1:T(1,128)S(1)} all-to-all(f32[1,256,512]{2,0,1:T(1,128)S(1)} %copy.728), channel_id=1, replica_groups=mesh['row'=8,'col'=4] {'col'}, dimensions={1} | all-to-all | bytes 1048576 | tf_op jit(solution)/shard_map/all_to_all | solution.py:194
  794.6 6.4 all-to-all-start.14
  803.5 6.5 all-to-all-done.14
  824.3 10.6 reduce.46
  842.1 10.4 reduce.44
  892.2 10.6 reduce.48
  907.7 9.0 fusion.811
  916.7 34.8 %reshape_squeeze.7 = f32[128,2,256,2]{3,2,1,0:T(8,128)} reshape(f32[1,4,64,512]{3,2,1,0:T(8,128)S(1)} %copy-done.25) | data formatting | bytes 1048576 | tf_op jit(solution)/shard_map/reshape;squeeze | solution.py:38
  951.5 13.3 %reduce_sum.29 = f32[128,256]{1,0:T(8,128)S(1)} reduce(f32[128,2,256,2]{3,2,1,0:T(8,128)} %reshape_squeeze.7, f32[]{:T(128)} %constant.215.clone.1), dimensions={1,3}, to_apply=%region_2.3 | reduce | flops 98304 | bytes 655364 | tf_op jit(solution)/shard_map/reduce_sum | solution.py:38
  964.8 34.9 %reshape_squeeze.6 = f32[128,2,256,2]{3,2,1,0:T(8,128)} reshape(f32[1,4,64,512]{3,2,1,0:T(8,128)S(1)} %copy-done.24) | data formatting | bytes 1048576 | tf_op jit(solution)/shard_map/reshape;squeeze | solution.py:38
  999.7 13.3 %reduce_sum.28 = f32[128,256]{1,0:T(8,128)S(1)} reduce(f32[128,2,256,2]{3,2,1,0:T(8,128)} %reshape_squeeze.6, f32[]{:T(128)} %constant.215.clone.1), dimensions={1,3}, to_apply=%region_1.2 | reduce | flops 98304 | bytes 655364 | tf_op jit(solution)/shard_map/reduce_sum | solution.py:38
  1027.5 35.6 %reshape.1180 = f32[128,2,256,2]{3,2,1,0:T(8,128)} reshape(f32[256,512]{1,0:T(8,128)} %get-tuple-element.29) | data formatting | bytes 1048576 | tf_op jit(solution)/shard_map/reshape | solution.py:38
  1063.1 13.2 %reduce_sum.27 = f32[128,256]{1,0:T(8,128)S(1)} reduce(f32[128,2,256,2]{3,2,1,0:T(8,128)} %reshape.1180, f32[]{:T(128)} %constant.215.clone.1), dimensions={1,3}, to_apply=%region_0.1 | reduce | flops 98304 | bytes 655364 | tf_op jit(solution)/shard_map/reduce_sum | solution.py:38
  1114.3 12.8 %fusion.26 = f32[1,16,128,256]{3,2,1,0:T(8,128)} fusion(f32[49,1,256]{2,1,0:T(1,128)S(1)} %copy-done.32, f32[1,128,256]{2,1,0:T(8,128)S(1)} %multiply_bitcast_fusion.2, f32[48,128,256]{2,1,0:T(8,128)S(1)} %bitcast.781, f32[49,1,256]{2,1,0:T(1,128)S(1)} %copy-done.30, f32[49,130,1]{2,1,0:T(8,128)S(1)} %copy-done, f32[49,130,1]{2,1,0:T(8,128)S(1)} %copy-done.1, ...), kind=kLoop, calls=%fused_computation.37 | loop fusion | flops 27787264 | bytes 19419024 | tf_op jit(solution)/shard_map/stack | solution.py:84
  1127.2 11.0 fusion.37
  1138.2 11.5 fusion.31
  (390 shorter events, 461.4 us)
Async XLA Ops:
  5.4 32.1 %all-to-all-start = ((f32[2,256,512]{2,0,1:T(2,128)}), f32[2,256,512]{2,0,1:T(2,128)S(1)}, u32[]{:S(2)}, u32[]{:S(2)}) async-start(f32[2,256,512]{2,0,1:T(2,128)} %pad_maximum_fusion.27), calls=%async_computation | async-start | bytes 2097152 | tf_op jit(solution)/shard_map/all_to_all | solution.py:194
  11.7 29.6 %copy-start.49 = (f32[22]{0:T(128)}, f32[22]{0:T(128)S(1)}, u32[]{:S(2)}) copy-start(f32[22]{0:T(128)S(1)} %compare_convert_fusion) | copy-start | bytes 268
  47.2 6.8 copy-start.5
  78.2 22.6 %all-to-all-start.1 = ((f32[32,1,2816]{2,1,0:T(1,128)}), f32[32,1,2816]{2,1,0:T(1,128)S(1)}, u32[]{:S(2)}, u32[]{:S(2)}) async-start(f32[32,1,2816]{2,1,0:T(1,128)} %reshape.1231), calls=%async_computation.1 | async-start | bytes 720896 | tf_op jit(solution)/shard_map/all_to_all | solution.py:197
  100.8 17.3 %all-to-all-start.2 = ((f32[32,1,2816]{2,1,0:T(1,128)}), f32[32,1,2816]{2,1,0:T(1,128)S(1)}, u32[]{:S(2)}, u32[]{:S(2)}) async-start(f32[32,1,2816]{2,1,0:T(1,128)} %reshape.1233), calls=%async_computation.2 | async-start | bytes 720896 | tf_op jit(solution)/shard_map/all_to_all | solution.py:200
  144.1 5.4 copy-start.45
  157.7 5.7 copy-start.44
  157.7 5.8 copy-start.43
  164.2 4.6 copy-start.13
  200.5 33.4 %all-to-all-start.3 = ((f32[32,1,9856]{2,1,0:T(1,128)}), f32[32,1,9856]{2,1,0:T(1,128)}, u32[]{:S(2)}, u32[]{:S(2)}) async-start(f32[32,1,9856]{2,1,0:T(1,128)} %reshape.1235), calls=%async_computation.3 | async-start | bytes 2523136 | tf_op jit(solution)/shard_map/all_to_all | solution.py:212
  233.9 34.2 %all-to-all-start.4 = ((f32[32,1,9856]{2,1,0:T(1,128)}), f32[32,1,9856]{2,1,0:T(1,128)}, u32[]{:S(2)}, u32[]{:S(2)}) async-start(f32[32,1,9856]{2,1,0:T(1,128)} %reshape.1237), calls=%async_computation.4 | async-start | bytes 2523136 | tf_op jit(solution)/shard_map/all_to_all | solution.py:213
  239.0 100.5 %copy-start.47 = (f32[32,64]{0,1:T(8,128)}, f32[32,64]{0,1:T(8,128)S(1)}, u32[]{:S(2)}) copy-start(f32[32,64]{0,1:T(8,128)S(1)} %copy.677) | copy-start | bytes 24580
  361.8 12.5 %copy-start.4 = (f32[7,32,64,64]{3,1,2,0:T(8,128)S(1)}, f32[7,32,64,64]{3,1,2,0:T(8,128)}, u32[]{:S(2)}) copy-start(f32[7,32,64,64]{3,1,2,0:T(8,128)} %get-tuple-element.32) | copy-start | bytes 11010052
  532.7 20.9 %copy-start.19 = (f32[1,4,64,512]{3,2,1,0:T(8,128)}, f32[1,4,64,512]{3,2,1,0:T(8,128)S(1)}, u32[]{:S(2)}) copy-start(f32[1,4,64,512]{3,2,1,0:T(8,128)S(1)} %get-tuple-element.55) | copy-start | bytes 1572868
  534.2 19.2 %all-to-all-start.6 = ((f32[1,256,512]{2,0,1:T(1,128)}), f32[1,256,512]{2,0,1:T(1,128)S(1)}, u32[]{:S(2)}, u32[]{:S(2)}) async-start(f32[1,256,512]{2,0,1:T(1,128)} %copy.684), calls=%async_computation.6 | async-start | bytes 1048576 | tf_op jit(solution)/shard_map/all_to_all | solution.py:194
  558.6 7.0 copy-start.14
  568.7 15.4 %all-to-all-start.7 = ((f32[32,1,1408]{2,1,0:T(1,128)}), f32[32,1,1408]{2,1,0:T(1,128)S(1)}, u32[]{:S(2)}, u32[]{:S(2)}) async-start(f32[32,1,1408]{2,1,0:T(1,128)} %reshape.1241), calls=%async_computation.7 | async-start | bytes 360448 | tf_op jit(solution)/shard_map/all_to_all | solution.py:197
  584.1 15.2 %all-to-all-start.8 = ((f32[32,1,1408]{2,1,0:T(1,128)}), f32[32,1,1408]{2,1,0:T(1,128)S(1)}, u32[]{:S(2)}, u32[]{:S(2)}) async-start(f32[32,1,1408]{2,1,0:T(1,128)} %reshape.1243), calls=%async_computation.8 | async-start | bytes 360448 | tf_op jit(solution)/shard_map/all_to_all | solution.py:200
  620.4 14.2 %all-to-all-start.10 = ((f32[32,1,2816]{2,1,0:T(1,128)}), f32[32,1,2816]{2,1,0:T(1,128)S(1)}, u32[]{:S(2)}, u32[]{:S(2)}) async-start(f32[32,1,2816]{2,1,0:T(1,128)} %reshape.1245), calls=%async_computation.10 | async-start | bytes 720896 | tf_op jit(solution)/shard_map/all_to_all | solution.py:213
  634.6 17.7 %all-to-all-start.9 = ((f32[32,1,2816]{2,1,0:T(1,128)}), f32[32,1,2816]{2,1,0:T(1,128)S(1)}, u32[]{:S(2)}, u32[]{:S(2)}) async-start(f32[32,1,2816]{2,1,0:T(1,128)} %reshape.1247), calls=%async_computation.9 | async-start | bytes 720896 | tf_op jit(solution)/shard_map/all_to_all | solution.py:212
  770.3 7.0 copy-start.15
  780.5 14.1 %all-to-all-start.13 = ((f32[32,1,1408]{2,1,0:T(1,128)}), f32[32,1,1408]{2,1,0:T(1,128)S(1)}, u32[]{:S(2)}, u32[]{:S(2)}) async-start(f32[32,1,1408]{2,1,0:T(1,128)} %reshape.1251), calls=%async_computation.13 | async-start | bytes 360448 | tf_op jit(solution)/shard_map/all_to_all | solution.py:197
  794.6 15.4 %all-to-all-start.14 = ((f32[32,1,1408]{2,1,0:T(1,128)}), f32[32,1,1408]{2,1,0:T(1,128)S(1)}, u32[]{:S(2)}, u32[]{:S(2)}) async-start(f32[32,1,1408]{2,1,0:T(1,128)} %reshape.1253), calls=%async_computation.14 | async-start | bytes 360448 | tf_op jit(solution)/shard_map/all_to_all | solution.py:200
  836.6 17.6 %all-to-all-start.15 = ((f32[32,1,1408]{2,1,0:T(1,128)}), f32[32,1,1408]{2,1,0:T(1,128)S(1)}, u32[]{:S(2)}, u32[]{:S(2)}) async-start(f32[32,1,1408]{2,1,0:T(1,128)} %reshape.1255), calls=%async_computation.15 | async-start | bytes 360448 | tf_op jit(solution)/shard_map/all_to_all | solution.py:212
  854.2 15.1 %all-to-all-start.16 = ((f32[32,1,1408]{2,1,0:T(1,128)}), f32[32,1,1408]{2,1,0:T(1,128)S(1)}, u32[]{:S(2)}, u32[]{:S(2)}) async-start(f32[32,1,1408]{2,1,0:T(1,128)} %reshape.1257), calls=%async_computation.16 | async-start | bytes 360448 | tf_op jit(solution)/shard_map/all_to_all | solution.py:213
  904.2 110.5 %all-to-all-start.17 = ((f32[4,1,32768]{2,1,0:T(1,128)}), f32[4,1,32768]{2,1,0:T(1,128)S(1)}, u32[]{:S(2)}, u32[]{:S(2)}) async-start(f32[4,1,32768]{2,1,0:T(1,128)} %reshape.1259), calls=%async_computation.17 | async-start | bytes 1048576 | tf_op jit(solution)/shard_map/all_to_all | solution.py:217
  907.7 9.0 copy-start.25
  951.5 13.3 %copy-start.24 = (f32[1,4,64,512]{3,2,1,0:T(8,128)S(1)}, f32[1,4,64,512]{3,2,1,0:T(8,128)}, u32[]{:S(2)}) copy-start(f32[1,4,64,512]{3,2,1,0:T(8,128)} %get-tuple-element.51) | copy-start | bytes 1572868
  999.7 14.0 %copy-start.26 = (f32[1,4,64,512]{3,1,2,0:T(4,128)S(1)}, f32[1,4,64,512]{3,1,2,0:T(4,128)}, u32[]{:S(2)}) copy-start(f32[1,4,64,512]{3,1,2,0:T(4,128)} %get-tuple-element.66) | copy-start | bytes 1572868
  1017.6 7.0 copy-start.18
  1017.6 7.0 copy-start.20
  1017.6 7.0 copy-start.22
  1077.6 4.7 collective-permute-start
  1077.7 4.6 collective-permute-start.1
  1093.9 9.3 collective-permute-start.2
  1100.7 6.1 collective-permute-start.3
  1109.3 4.8 copy-start.7
  1109.4 4.9 copy-start.33
  1109.4 4.9 copy-start.36
  1109.4 4.9 copy-start.37
  1109.4 4.9 copy-start.51
  1114.3 12.8 %copy-start.8 = (f32[15,128,256]{2,1,0:T(8,128)S(1)}, f32[15,128,256]{2,1,0:T(8,128)}, u32[]{:S(2)}) copy-start(f32[15,128,256]{2,1,0:T(8,128)} %get-tuple-element.41) | copy-start | bytes 5898244
  1114.3 12.8 %copy-start.9 = (f32[15,128,256]{2,1,0:T(8,128)S(1)}, f32[15,128,256]{2,1,0:T(8,128)}, u32[]{:S(2)}) copy-start(f32[15,128,256]{2,1,0:T(8,128)} %get-tuple-element.42) | copy-start | bytes 5898244
  1114.3 12.8 %copy-start.34 = (f32[1,128,256]{2,1,0:T(8,128)S(1)}, f32[1,128,256]{2,1,0:T(8,128)}, u32[]{:S(2)}) copy-start(f32[1,128,256]{2,1,0:T(8,128)} %get-tuple-element.76) | copy-start | bytes 393220
  1114.3 12.8 %copy-start.35 = (f32[128,256]{1,0:T(8,128)S(1)}, f32[128,256]{1,0:T(8,128)}, u32[]{:S(2)}) copy-start(f32[128,256]{1,0:T(8,128)} %get-tuple-element.77) | copy-start | bytes 393220
  1114.3 12.8 %copy-start.38 = (f32[1,128,256]{2,1,0:T(8,128)S(1)}, f32[1,128,256]{2,1,0:T(8,128)}, u32[]{:S(2)}) copy-start(f32[1,128,256]{2,1,0:T(8,128)} %get-tuple-element.46) | copy-start | bytes 393220
  1127.1 11.1 copy-start.10
  1127.2 11.0 copy-start.46
  (25 other events, 60.4 us)
where the time goes:
time: 1160 us
  local copies, waits for them, and re-layouts  392 us (34%)
  matrix products  270 us (23%)
  other arithmetic  200 us (17%)
  blocking collectives  136 us (12%)
  waiting for transfers between devices  80.1 us (7%)
  starting transfers between devices  75.2 us (6%)
    dot_general x84, matrix products, product(): return jnp.einsum(form, left, right, precision=lax.Precision.HIGHEST)  270 us
    all_to_all x2, blocking collectives, inverse(): lax.all_to_all(pencil, 'col', split_axis=2, concat_axis=1, tiled=True)  119 us
    unnamed x150, local copies, waits for them, and re-layouts  111 us
    another operation x2, local copies, waits for them, and re-layouts, coarsen(): return source.reshape(rows_out, COARSE, cols_out, COARSE).mean(axis=(1, 3))  69.7 us
    another operation x4, other arithmetic, flow_update(): return jnp.stack([next_u, next_v, next_w])  41.6 us
    all_to_all x2, waiting for transfers between devices, forward(): lax.all_to_all(stacked, 'col', split_axis=1, concat_axis=2, tiled=True)  40.8 us
    reduce_sum x3, other arithmetic, coarsen(): return source.reshape(rows_out, COARSE, cols_out, COARSE).mean(axis=(1, 3))  39.8 us
    unnamed x8, other arithmetic  37.8 us
  transfers between devices with their start and end apart: 19, of which 11 were waited for; matrix products, arithmetic and copies ran while one was open for 22% of the time, Pallas kernels for 0%

commit v1 on v0

--- a/solution.py
+++ b/solution.py
@@ -214,7 +214,10 @@
         )
         full_real, full_imag = unfold_half(full_real, full_imag, kept_modes)
         pencil = transform(full_real, full_imag, 1.0, "back", True) / float(NX * NY)
-        return lax.all_to_all(pencil, "col", split_axis=2, concat_axis=1, tiled=True)
+        return jnp.concatenate(
+            lax.all_to_all(jnp.stack(jnp.split(pencil, lax.axis_size("col"), axis=2)), "col", 0, 0),
+            axis=1,
+        )
 
     first_real, first_imag = forward(jnp.stack([surface_potential, surface_height]))
     pot_hat = (first_real[0], first_imag[0])

time: 1160 us -> 1080 us (0.931)
  local copies, waits for them, and re-layouts: 392 us -> 338 us
  other arithmetic: 200 us -> 171 us
    unnamed x150 -> x142, local copies, waits for them, and re-layouts: 111 us -> 82 us
    div x5 -> x3, local copies, waits for them, and re-layouts: 28.7 us -> 6.14 us  [inverse(): pencil = transform(full_real, full_imag, 1.0, 'back', True) / float(NX * NY)]
    all_to_all x3 -> x0, other arithmetic: 21.3 us -> none  [inverse(): lax.all_to_all(pencil, 'col', split_axis=2, concat_axis=1, tiled=True)]
    all_to_all x4 -> x2, local copies, waits for them, and re-layouts: 12.9 us -> 0.67 us  [inverse(): lax.all_to_all(jnp.stack(jnp.split(pencil, lax.axis_size('col'), axis=2))...]
    unnamed x8 -> x7, other arithmetic: 37.8 us -> 27 us
  transfers between devices with their start and end apart: 19 -> 19, of which waited for: 11 -> 11; matrix products, arithmetic and copies ran while one was open for 22% -> 24% of each run, Pallas kernels for 0% -> 0%
where the time goes in v1:
time: 1080 us; the launch traced here: 1070 us
  local copies, waits for them, and re-layouts  338 us (31%)
  matrix products  270 us (25%)
  other arithmetic  171 us (16%)
  blocking collectives  134 us (12%)
  waiting for transfers between devices  79.7 us (7%)
  starting transfers between devices  75.7 us (7%)
    dot_general x84, matrix products, product(): return jnp.einsum(form, left, right, precision=lax.Precision.HIGHEST)  270 us
    all_to_all x2, blocking collectives, inverse(): lax.all_to_all(jnp.stack(jnp.split(pencil, lax.axis_size('col'), axis=2))...  117 us
    unnamed x142, local copies, waits for them, and re-layouts  82 us
    another operation x2, local copies, waits for them, and re-layouts, coarsen(): return source.reshape(rows_out, COARSE, cols_out, COARSE).mean(axis=(1, 3))  69.6 us
    another operation x4, other arithmetic, flow_update(): return jnp.stack([next_u, next_v, next_w])  41.6 us
    all_to_all x2, waiting for transfers between devices, forward(): lax.all_to_all(stacked, 'col', split_axis=1, concat_axis=2, tiled=True)  40.3 us
    reduce_sum x3, other arithmetic, coarsen(): return source.reshape(rows_out, COARSE, cols_out, COARSE).mean(axis=(1, 3))  39.9 us
    reshape x1, local copies, waits for them, and re-layouts, coarsen(): return source.reshape(rows_out, COARSE, cols_out, COARSE).mean(axis=(1, 3))  35.6 us
  transfers between devices with their start and end apart: 19, of which 11 were waited for; matrix products, arithmetic and copies ran while one was open for 24% of the time, Pallas kernels for 0%

profile of v1, /device:TPU:0, one launch (start us, length us, event | category | flops | bytes accessed | tf_op | source)
XLA Modules:
  0.0 1070.5 jit_solution(11088245342983798772)
XLA Ops:
  5.4 6.3 all-to-all-start
  12.0 25.5 %all-to-all-done = f32[2,256,512]{2,0,1:T(2,128)S(1)} async-done(((f32[2,256,512]{2,0,1:T(2,128)}), f32[2,256,512]{2,0,1:T(2,128)S(1)}, u32[]{:S(2)}, u32[]{:S(2)}) %all-to-all-start) | async-done | bytes 1048608 | tf_op jit(solution)/shard_map/all_to_all | solution.py:194
  47.2 6.8 fusion.71
  54.0 18.9 %subtract_bitcast_fusion.3 = f32[2,64,32,64]{3,1,2,0:T(8,128)S(1)} fusion(f32[64,2,64,32]{2,0,3,1:T(8,128)S(1)} %fusion.71, f32[2,64,32,64]{3,2,1,0:T(8,128)S(1)} %get-tuple-element.53), kind=kOutput, calls=%fused_computation.120 | convolution fusion | flops 201646080 | bytes 3145728 | tf_op jit(solution)/shard_map/bmkn,nq->bqkm/dot_general | solution.py:88
  81.9 8.4 fusion.69
  90.2 6.8 add_bitcast_fusion.3
  111.7 6.4 all-to-all-done.2
  134.8 9.1 multiply_reduce_fusion.4
  183.9 8.7 copy.643
  192.6 8.0 reshape.1244
  212.8 8.7 copy.648
  221.5 8.0 reshape.1246
  244.0 6.0 reshape.1245
  250.1 6.5 copy.496
  259.0 9.2 all-to-all-done.4
  268.2 6.0 reduce.30
  274.2 7.1 reshape.1247
  281.3 6.5 copy.504
  294.1 14.8 %fusion.4 = f32[32,7,64,64]{3,0,2,1:T(8,128)} fusion(f32[7,32,64,64]{3,2,1,0:T(8,128)S(1)} %bitcast.796), kind=kOutput, calls=%fused_computation.8 | convolution fusion | flops 352335872 | bytes 7340032 | tf_op jit(solution)/shard_map/banm,ak->bknm/dot_general | solution.py:88
  308.9 14.8 %fusion.6 = f32[32,7,64,64]{3,0,2,1:T(8,128)} fusion(f32[7,32,64,64]{3,2,1,0:T(8,128)S(1)} %bitcast.797), kind=kOutput, calls=%fused_computation.10 | convolution fusion | flops 352335872 | bytes 7340032 | tf_op jit(solution)/shard_map/banm,ak->bknm/dot_general | solution.py:88
  324.3 15.1 %fusion.8 = f32[32,7,64,64]{3,0,2,1:T(8,128)} fusion(f32[7,32,64,64]{3,2,1,0:T(8,128)S(1)} %bitcast.798), kind=kOutput, calls=%fused_computation.12 | convolution fusion | flops 352335872 | bytes 7340032 | tf_op jit(solution)/shard_map/banm,ak->bknm/dot_general | solution.py:88
  339.4 22.3 %subtract_bitcast_fusion = (f32[7,32,64,64]{3,1,2,0:T(8,128)}, f32[7,32,64,64]{3,1,2,0:T(8,128)}) fusion(f32[32,64]{0,1:T(8,128)S(1)} %copy.510, f32[32,64]{0,1:T(8,128)S(1)} %copy.507, f32[32,7,64,64]{3,0,2,1:T(8,128)} %fusion.8, f32[32,7,64,64]{3,0,2,1:T(8,128)} %fusion.4, f32[32,7,64,64]{3,0,2,1:T(8,128)} %fusion.6, f32[7,32,64,64]{3,2,1,0:T(8,128)S(1)} %bitcast.799), kind=kOutput, calls=%fused_computation.7 | convolution fusion | flops 359675904 | bytes 22036480 | tf_op jit(solution)/shard_map/banm,ak->bknm/dot_general | solution.py:88
  361.7 12.7 %fusion = f32[64,7,32,64]{3,0,2,1:T(8,128)S(1)} fusion(f32[7,32,64,64]{3,1,2,0:T(8,128)} %get-tuple-element.33), kind=kOutput, calls=%fused_computation.1 | convolution fusion | flops 704700416 | bytes 7340032 | tf_op jit(solution)/shard_map/bknm,nq->bmqk/dot_general | solution.py:88
  374.3 11.4 %multiply_bitcast_fusion = f32[7,64,64,32]{1,2,3,0:T(8,128)S(1)} fusion(f32[64,7,32,64]{3,0,2,1:T(8,128)S(1)} %fusion, f32[7,32,64,64]{3,1,2,0:T(8,128)S(1)} %copy-done.4), kind=kOutput, calls=%fused_computation.5 | convolution fusion | flops 706535424 | bytes 11010048 | tf_op jit(solution)/shard_map/bknm,nq->bmqk/dot_general | solution.py:88
  394.2 6.2 copy.514
  400.5 87.8 %all_to_all.258 = f32[4,7,64,512]{3,2,1,0:T(8,128)S(1)} all-to-all(f32[4,7,64,512]{3,2,1,0:T(8,128)} %copy.514), channel_id=1, replica_groups=mesh['row'=8,'col'=4] {'col'}, dimensions={0} | all-to-all | bytes 7340032 | tf_op jit(solution)/shard_map/all_to_all | solution.py:218
  495.8 14.8 %all-to-all-done.6 = f32[1,256,512]{2,0,1:T(1,128)S(1)} async-done(((f32[1,256,512]{2,0,1:T(1,128)}), f32[1,256,512]{2,0,1:T(1,128)S(1)}, u32[]{:S(2)}, u32[]{:S(2)}) %all-to-all-start.6) | async-done | bytes 524320 | tf_op jit(solution)/shard_map/all_to_all | solution.py:194
  540.4 6.4 all-to-all-start.8
  549.3 6.5 all-to-all-done.8
  591.0 6.0 all-to-all-start.9
  652.7 29.6 %all_to_all.259 = f32[4,2,64,512]{3,2,1,0:T(8,128)S(1)} all-to-all(f32[4,2,64,512]{3,2,1,0:T(8,128)S(1)} %copy.557), channel_id=1, replica_groups=mesh['row'=8,'col'=4] {'col'}, dimensions={0} | all-to-all | bytes 2097152 | tf_op jit(solution)/shard_map/all_to_all | solution.py:218
  684.1 16.6 %all_to_all.260 = f32[1,256,512]{2,0,1:T(1,128)S(1)} all-to-all(f32[1,256,512]{2,0,1:T(1,128)S(1)} %copy.559), channel_id=1, replica_groups=mesh['row'=8,'col'=4] {'col'}, dimensions={1} | all-to-all | bytes 1048576 | tf_op jit(solution)/shard_map/all_to_all | solution.py:194
  731.0 6.1 all-to-all-start.14
  739.6 6.5 all-to-all-done.14
  760.4 10.6 reduce.44
  778.2 10.4 reduce.42
  790.2 6.2 all-to-all-start.16
  832.8 9.0 fusion.811
  841.8 34.8 %reshape_squeeze.7 = f32[128,2,256,2]{3,2,1,0:T(8,128)} reshape(f32[1,4,64,512]{3,2,1,0:T(8,128)S(1)} %copy-done.25) | data formatting | bytes 1048576 | tf_op jit(solution)/shard_map/reshape;squeeze | solution.py:38
  876.6 13.3 %reduce_sum.29 = f32[128,256]{1,0:T(8,128)S(1)} reduce(f32[128,2,256,2]{3,2,1,0:T(8,128)} %reshape_squeeze.7, f32[]{:T(128)} %constant.215.clone.1), dimensions={1,3}, to_apply=%region_2.3 | reduce | flops 98304 | bytes 655364 | tf_op jit(solution)/shard_map/reduce_sum | solution.py:38
  889.9 34.8 %reshape_squeeze.6 = f32[128,2,256,2]{3,2,1,0:T(8,128)} reshape(f32[1,4,64,512]{3,2,1,0:T(8,128)S(1)} %copy-done.24) | data formatting | bytes 1048576 | tf_op jit(solution)/shard_map/reshape;squeeze | solution.py:38
  924.7 13.3 %reduce_sum.28 = f32[128,256]{1,0:T(8,128)S(1)} reduce(f32[128,2,256,2]{3,2,1,0:T(8,128)} %reshape_squeeze.6, f32[]{:T(128)} %constant.215.clone.1), dimensions={1,3}, to_apply=%region_1.2 | reduce | flops 98304 | bytes 655364 | tf_op jit(solution)/shard_map/reduce_sum | solution.py:38
  942.0 35.6 %reshape.1189 = f32[128,2,256,2]{3,2,1,0:T(8,128)} reshape(f32[256,512]{1,0:T(8,128)} %get-tuple-element.29) | data formatting | bytes 1048576 | tf_op jit(solution)/shard_map/reshape | solution.py:38
  977.5 13.2 %reduce_sum.27 = f32[128,256]{1,0:T(8,128)S(1)} reduce(f32[128,2,256,2]{3,2,1,0:T(8,128)} %reshape.1189, f32[]{:T(128)} %constant.215.clone.1), dimensions={1,3}, to_apply=%region_0.1 | reduce | flops 98304 | bytes 655364 | tf_op jit(solution)/shard_map/reduce_sum | solution.py:38
  1028.6 12.8 %fusion.26 = f32[1,16,128,256]{3,2,1,0:T(8,128)} fusion(f32[49,1,256]{2,1,0:T(1,128)S(1)} %copy-done.31, f32[1,128,256]{2,1,0:T(8,128)S(1)} %multiply_bitcast_fusion.2, f32[48,128,256]{2,1,0:T(8,128)S(1)} %bitcast.793, f32[49,1,256]{2,1,0:T(1,128)S(1)} %copy-done.29, f32[49,130,1]{2,1,0:T(8,128)S(1)} %copy-done, f32[49,130,1]{2,1,0:T(8,128)S(1)} %copy-done.1, ...), kind=kLoop, calls=%fused_computation.39 | loop fusion | flops 27787264 | bytes 19419024 | tf_op jit(solution)/shard_map/stack | solution.py:84
  1041.5 11.0 %fusion.37 = f32[1,16,128,256]{3,2,1,0:T(8,128)} fusion(f32[49,1,256]{2,1,0:T(1,128)S(1)} %copy-done.31, f32[1,128,256]{2,1,0:T(8,128)S(1)} %multiply_bitcast_fusion.2, f32[48,128,256]{2,1,0:T(8,128)S(1)} %bitcast.794, f32[49,1,256]{2,1,0:T(1,128)S(1)} %copy-done.29, f32[3,16,128,256]{3,2,1,0:T(8,128)S(1)} %bitcast.792, f32[1,128,256]{2,1,0:T(8,128)S(1)} %copy-done.37, ...), kind=kLoop, calls=%fused_computation.50 | loop fusion | flops 26214400 | bytes 19419024 | tf_op jit(solution)/shard_map/stack | solution.py:84
  1052.5 11.5 %fusion.31 = f32[1,16,128,256]{3,2,1,0:T(8,128)} fusion(f32[1,128,256]{2,1,0:T(8,128)S(1)} %copy-done.45, f32[15,128,256]{2,1,0:T(8,128)} %get-tuple-element.43, f32[15,128,256]{2,1,0:T(8,128)} %get-tuple-element.44, f32[49,1,256]{2,1,0:T(1,128)S(1)} %copy-done.31, f32[1,128,256]{2,1,0:T(8,128)S(1)} %multiply_bitcast_fusion.2, ...), kind=kLoop, calls=%fused_computation.44 | loop fusion | flops 27262976 | bytes 27676496 | tf_op jit(solution)/shard_map/stack | solution.py:84
  1064.0 6.3 pad_maximum_fusion.2
  (381 shorter events, 404.3 us)
Async XLA Ops:
  5.4 32.1 %all-to-all-start = ((f32[2,256,512]{2,0,1:T(2,128)}), f32[2,256,512]{2,0,1:T(2,128)S(1)}, u32[]{:S(2)}, u32[]{:S(2)}) async-start(f32[2,256,512]{2,0,1:T(2,128)} %pad_maximum_fusion.29), calls=%async_computation | async-start | bytes 2097152 | tf_op jit(solution)/shard_map/all_to_all | solution.py:194
  11.7 29.6 %copy-start.48 = (f32[22]{0:T(128)}, f32[22]{0:T(128)S(1)}, u32[]{:S(2)}) copy-start(f32[22]{0:T(128)S(1)} %compare_convert_fusion) | copy-start | bytes 268
  47.2 6.8 copy-start.5
  78.2 22.6 %all-to-all-start.1 = ((f32[32,1,2816]{2,1,0:T(1,128)}), f32[32,1,2816]{2,1,0:T(1,128)S(1)}, u32[]{:S(2)}, u32[]{:S(2)}) async-start(f32[32,1,2816]{2,1,0:T(1,128)} %reshape.1240), calls=%async_computation.1 | async-start | bytes 720896 | tf_op jit(solution)/shard_map/all_to_all | solution.py:197
  100.8 17.3 %all-to-all-start.2 = ((f32[32,1,2816]{2,1,0:T(1,128)}), f32[32,1,2816]{2,1,0:T(1,128)S(1)}, u32[]{:S(2)}, u32[]{:S(2)}) async-start(f32[32,1,2816]{2,1,0:T(1,128)} %reshape.1242), calls=%async_computation.2 | async-start | bytes 720896 | tf_op jit(solution)/shard_map/all_to_all | solution.py:200
  144.1 5.4 copy-start.44
  157.7 5.7 copy-start.43
  157.7 5.8 copy-start.42
  164.2 4.6 copy-start.13
  168.8 4.3 copy-start.12
  200.6 33.4 %all-to-all-start.3 = ((f32[32,1,9856]{2,1,0:T(1,128)}), f32[32,1,9856]{2,1,0:T(1,128)}, u32[]{:S(2)}, u32[]{:S(2)}) async-start(f32[32,1,9856]{2,1,0:T(1,128)} %reshape.1244), calls=%async_computation.3 | async-start | bytes 2523136 | tf_op jit(solution)/shard_map/all_to_all | solution.py:212
  234.0 34.2 %all-to-all-start.4 = ((f32[32,1,9856]{2,1,0:T(1,128)}), f32[32,1,9856]{2,1,0:T(1,128)}, u32[]{:S(2)}, u32[]{:S(2)}) async-start(f32[32,1,9856]{2,1,0:T(1,128)} %reshape.1246), calls=%async_computation.4 | async-start | bytes 2523136 | tf_op jit(solution)/shard_map/all_to_all | solution.py:213
  239.1 100.3 %copy-start.46 = (f32[32,64]{0,1:T(8,128)}, f32[32,64]{0,1:T(8,128)S(1)}, u32[]{:S(2)}) copy-start(f32[32,64]{0,1:T(8,128)S(1)} %copy.510) | copy-start | bytes 24580
  361.7 12.7 %copy-start.4 = (f32[7,32,64,64]{3,1,2,0:T(8,128)S(1)}, f32[7,32,64,64]{3,1,2,0:T(8,128)}, u32[]{:S(2)}) copy-start(f32[7,32,64,64]{3,1,2,0:T(8,128)} %get-tuple-element.32) | copy-start | bytes 11010052
  490.8 20.1 %copy-start.19 = (f32[1,4,64,512]{3,2,1,0:T(8,128)}, f32[1,4,64,512]{3,2,1,0:T(8,128)S(1)}, u32[]{:S(2)}) copy-start(f32[1,4,64,512]{3,2,1,0:T(8,128)S(1)} %get-tuple-element.59) | copy-start | bytes 1572868
  492.3 18.3 %all-to-all-start.6 = ((f32[1,256,512]{2,0,1:T(1,128)}), f32[1,256,512]{2,0,1:T(1,128)S(1)}, u32[]{:S(2)}, u32[]{:S(2)}) async-start(f32[1,256,512]{2,0,1:T(1,128)} %copy.516), calls=%async_computation.6 | async-start | bytes 1048576 | tf_op jit(solution)/shard_map/all_to_all | solution.py:194
  515.9 7.0 copy-start.14
  526.0 14.4 %all-to-all-start.7 = ((f32[32,1,1408]{2,1,0:T(1,128)}), f32[32,1,1408]{2,1,0:T(1,128)S(1)}, u32[]{:S(2)}, u32[]{:S(2)}) async-start(f32[32,1,1408]{2,1,0:T(1,128)} %reshape.1248), calls=%async_computation.7 | async-start | bytes 360448 | tf_op jit(solution)/shard_map/all_to_all | solution.py:197
  540.4 15.4 %all-to-all-start.8 = ((f32[32,1,1408]{2,1,0:T(1,128)}), f32[32,1,1408]{2,1,0:T(1,128)S(1)}, u32[]{:S(2)}, u32[]{:S(2)}) async-start(f32[32,1,1408]{2,1,0:T(1,128)} %reshape.1250), calls=%async_computation.8 | async-start | bytes 360448 | tf_op jit(solution)/shard_map/all_to_all | solution.py:200
  576.9 14.2 %all-to-all-start.10 = ((f32[32,1,2816]{2,1,0:T(1,128)}), f32[32,1,2816]{2,1,0:T(1,128)S(1)}, u32[]{:S(2)}, u32[]{:S(2)}) async-start(f32[32,1,2816]{2,1,0:T(1,128)} %reshape.1252), calls=%async_computation.10 | async-start | bytes 720896 | tf_op jit(solution)/shard_map/all_to_all | solution.py:213
  591.0 17.5 %all-to-all-start.9 = ((f32[32,1,2816]{2,1,0:T(1,128)}), f32[32,1,2816]{2,1,0:T(1,128)S(1)}, u32[]{:S(2)}, u32[]{:S(2)}) async-start(f32[32,1,2816]{2,1,0:T(1,128)} %reshape.1254), calls=%async_computation.9 | async-start | bytes 720896 | tf_op jit(solution)/shard_map/all_to_all | solution.py:212
  706.0 7.0 copy-start.15
  716.1 14.9 %all-to-all-start.13 = ((f32[32,1,1408]{2,1,0:T(1,128)}), f32[32,1,1408]{2,1,0:T(1,128)S(1)}, u32[]{:S(2)}, u32[]{:S(2)}) async-start(f32[32,1,1408]{2,1,0:T(1,128)} %reshape.1256), calls=%async_computation.13 | async-start | bytes 360448 | tf_op jit(solution)/shard_map/all_to_all | solution.py:197
  731.0 15.2 %all-to-all-start.14 = ((f32[32,1,1408]{2,1,0:T(1,128)}), f32[32,1,1408]{2,1,0:T(1,128)S(1)}, u32[]{:S(2)}, u32[]{:S(2)}) async-start(f32[32,1,1408]{2,1,0:T(1,128)} %reshape.1258), calls=%async_computation.14 | async-start | bytes 360448 | tf_op jit(solution)/shard_map/all_to_all | solution.py:200
  772.6 17.6 %all-to-all-start.15 = ((f32[32,1,1408]{2,1,0:T(1,128)}), f32[32,1,1408]{2,1,0:T(1,128)S(1)}, u32[]{:S(2)}, u32[]{:S(2)}) async-start(f32[32,1,1408]{2,1,0:T(1,128)} %reshape.1260), calls=%async_computation.15 | async-start | bytes 360448 | tf_op jit(solution)/shard_map/all_to_all | solution.py:212
  790.2 15.3 %all-to-all-start.16 = ((f32[32,1,1408]{2,1,0:T(1,128)}), f32[32,1,1408]{2,1,0:T(1,128)S(1)}, u32[]{:S(2)}, u32[]{:S(2)}) async-start(f32[32,1,1408]{2,1,0:T(1,128)} %reshape.1262), calls=%async_computation.16 | async-start | bytes 360448 | tf_op jit(solution)/shard_map/all_to_all | solution.py:213
  828.4 110.4 %all-to-all-start.17 = ((f32[4,1,64,512]{3,2,1,0:T(8,128)}), f32[4,1,64,512]{3,2,1,0:T(8,128)}, u32[]{:S(2)}, u32[]{:S(2)}) async-start(f32[4,1,64,512]{3,2,1,0:T(8,128)} %copy.600), calls=%async_computation.17 | async-start | bytes 1048576 | tf_op jit(solution)/shard_map/all_to_all | solution.py:218
  832.8 9.0 copy-start.25
  876.6 13.3 %copy-start.24 = (f32[1,4,64,512]{3,2,1,0:T(8,128)S(1)}, f32[1,4,64,512]{3,2,1,0:T(8,128)}, u32[]{:S(2)}) copy-start(f32[1,4,64,512]{3,2,1,0:T(8,128)} %get-tuple-element.55) | copy-start | bytes 1572868
  924.7 14.1 %copy-start.18 = (f32[1,4,64,512]{3,2,1,0:T(8,128)S(1)}, f32[1,4,64,512]{3,2,1,0:T(8,128)}, u32[]{:S(2)}) copy-start(f32[1,4,64,512]{3,2,1,0:T(8,128)} %get-tuple-element.62) | copy-start | bytes 1572868
  924.7 14.1 %copy-start.20 = (f32[1,4,64,512]{3,2,1,0:T(8,128)S(1)}, f32[1,4,64,512]{3,2,1,0:T(8,128)}, u32[]{:S(2)}) copy-start(f32[1,4,64,512]{3,2,1,0:T(8,128)} %copy-done.19) | copy-start | bytes 1572868
  924.7 14.1 %copy-start.22 = (f32[1,4,64,512]{3,2,1,0:T(8,128)S(1)}, f32[1,4,64,512]{3,2,1,0:T(8,128)}, u32[]{:S(2)}) copy-start(f32[1,4,64,512]{3,2,1,0:T(8,128)} %get-tuple-element.58) | copy-start | bytes 1572868
  992.0 4.8 collective-permute-start
  992.1 4.7 collective-permute-start.1
  1008.2 9.4 collective-permute-start.2
  1015.1 6.1 collective-permute-start.3
  1023.8 4.8 copy-start.7
  1023.8 4.8 copy-start.32
  1023.8 4.8 copy-start.35
  1023.8 4.8 copy-start.36
  1023.8 4.8 copy-start.50
  1028.6 12.8 %copy-start.8 = (f32[15,128,256]{2,1,0:T(8,128)S(1)}, f32[15,128,256]{2,1,0:T(8,128)}, u32[]{:S(2)}) copy-start(f32[15,128,256]{2,1,0:T(8,128)} %get-tuple-element.45) | copy-start | bytes 5898244
  1028.6 12.8 %copy-start.9 = (f32[15,128,256]{2,1,0:T(8,128)S(1)}, f32[15,128,256]{2,1,0:T(8,128)}, u32[]{:S(2)}) copy-start(f32[15,128,256]{2,1,0:T(8,128)} %get-tuple-element.46) | copy-start | bytes 5898244
  1028.6 12.8 %copy-start.33 = (f32[1,128,256]{2,1,0:T(8,128)S(1)}, f32[1,128,256]{2,1,0:T(8,128)}, u32[]{:S(2)}) copy-start(f32[1,128,256]{2,1,0:T(8,128)} %get-tuple-element.88) | copy-start | bytes 393220
  1028.6 12.8 %copy-start.34 = (f32[128,256]{1,0:T(8,128)S(1)}, f32[128,256]{1,0:T(8,128)}, u32[]{:S(2)}) copy-start(f32[128,256]{1,0:T(8,128)} %get-tuple-element.89) | copy-start | bytes 393220
  1028.6 12.8 %copy-start.37 = (f32[1,128,256]{2,1,0:T(8,128)S(1)}, f32[1,128,256]{2,1,0:T(8,128)}, u32[]{:S(2)}) copy-start(f32[1,128,256]{2,1,0:T(8,128)} %get-tuple-element.50) | copy-start | bytes 393220
  1041.5 11.0 %copy-start.10 = (f32[15,128,256]{2,1,0:T(8,128)S(1)}, f32[15,128,256]{2,1,0:T(8,128)}, u32[]{:S(2)}) copy-start(f32[15,128,256]{2,1,0:T(8,128)} %get-tuple-element.47) | copy-start | bytes 5898244
  1041.5 11.0 %copy-start.45 = (f32[1,128,256]{2,1,0:T(8,128)S(1)}, f32[1,128,256]{2,1,0:T(8,128)}, u32[]{:S(2)}) copy-start(f32[1,128,256]{2,1,0:T(8,128)} %get-tuple-element.49) | copy-start | bytes 393220
  (24 other events, 53.5 us)
